TPU v7x, 32 devices: a whole 2x2x4 slice. The times are simulated.
32 devices in a mesh: grp: 2 (over x), sp: 16 (over z, y, core).
Axes of the slice: x: 2, y: 2, z: 4, core: 2. Of those that a mesh axis runs over, the one named last changes fastest.
Arguments:
- video_query: bfloat16 [4, 16, 2048, 128], P('grp', None, 'sp'), parts along dimension 0, may hold values from -6 to 6
- video_key: bfloat16 [4, 16, 2048, 128], P('grp', None, 'sp'), parts along dimension 0, may hold values from -6 to 6
- video_value: bfloat16 [4, 16, 2048, 128], P('grp', None, 'sp'), parts along dimension 0, may hold values from -6 to 6
- text_query: bfloat16 [4, 16, 256, 128], P('grp', None, 'sp'), parts along dimension 0, may hold values from -6 to 6
- text_key: bfloat16 [4, 16, 256, 128], P('grp', None, 'sp'), parts along dimension 0, may hold values from -6 to 6
- text_value: bfloat16 [4, 16, 256, 128], P('grp', None, 'sp'), parts along dimension 0, may hold values from -6 to 6
- positions: int32 [6, 2048], P('grp', 'sp'), parts along dimension 0, may hold values from 0 to 63
- text_lengths: int32 [4], P('grp'), parts along dimension 0, may hold values from 1 to 256
- query_gain: float32 [128], replicated, may hold values from 1 to 2.2
- key_gain: float32 [128], replicated, may hold values from 1 to 2.2
- out_weight: bfloat16 [2048, 3072], replicated, may hold values from -0.125 to 0.125
- branch_gates: float32 [4, 3072], P('grp'), parts along dimension 0, may hold values from -3 to 3
- video_stream: bfloat16 [4, 2048, 3072], P('grp', 'sp'), parts along dimension 0, may hold values from -6 to 6
- text_stream: bfloat16 [4, 256, 3072], P('grp', 'sp'), parts along dimension 0, may hold values from -6 to 6
Outputs:
- guided: bfloat16 [2048, 6144], P('sp', 'grp'), parts along dimension 1
- video_next: bfloat16 [4, 2048, 3072], P('grp', 'sp'), parts along dimension 0
- text_next: bfloat16 [4, 256, 3072], P('grp', 'sp'), parts along dimension 0
There are 2 independent parts, one for each index of `grp`. A program takes and returns all parts, laid end to end along the dimension named above; an argument that names none is the same for every part. Nothing has to cross between parts.
Inputs may be any that keep to these rules, and one draw needn't show every extreme that they name: Entry 0 counts the conditional prompt's text tokens, entry 1 the unconditional one's; text tokens at index text_lengths[b] or later are padding.
All inputs are finite; a program needn't handle non-finite values.
Results may differ from a plain program's by a relative error of at most 0.0054.
Values may be sent and summed in bfloat16 or wider, within the bound.
A program may use at most 128 MiB of HBM per device.

v0:
```python
import math

import jax
import jax.numpy as jnp
from jax import lax
from jax.sharding import PartitionSpec as P

norm_eps = 1e-06
rope_theta = 256.0
guidance_scale = 5.0


def for_sending(value):

    def short(part):
        return part.astype(jnp.bfloat16) if part.dtype == jnp.float32 else part

    return jax.tree.map(short, value)


def rope_tables(positions, head_dim):
    frame_width = head_dim // 8
    side_width = 7 * head_dim // 16
    starts = (0, frame_width, frame_width + side_width)
    extents = (frame_width, side_width, side_width)
    channel = jnp.arange(head_dim, dtype=jnp.int32)
    angles = jnp.zeros((positions.shape[1], head_dim), jnp.float32)
    for axis_slot in range(3):
        inside = (channel >= starts[axis_slot]) & (channel < starts[axis_slot] + extents[axis_slot])
        within = ((channel - starts[axis_slot]) // 2).astype(jnp.float32)
        frequency = jnp.where(
            inside, jnp.exp(-2.0 * within / extents[axis_slot] * math.log(rope_theta)), 0.0
        ).astype(jnp.float32)
        angles = angles + positions[axis_slot].astype(jnp.float32)[:, None] * frequency[None, :]
    return (jnp.cos(angles), jnp.sin(angles))


def rms_scale(values, gain_vector):
    widened = values.astype(jnp.float32)
    return (
        widened
        * lax.rsqrt(jnp.mean(widened * widened, axis=-1, keepdims=True) + norm_eps)
        * gain_vector
    )


def rotate_pairs(values, cosine_table, sine_table):
    is_even = jnp.arange(values.shape[-1], dtype=jnp.int32) % 2 == 0
    partner = jnp.where(is_even, -jnp.roll(values, -1, axis=-1), jnp.roll(values, 1, axis=-1))
    return values * cosine_table + partner * sine_table


def prepare_rotated(values, gain_vector, cosine_table, sine_table):
    return rotate_pairs(rms_scale(values, gain_vector), cosine_table, sine_table).astype(
        jnp.bfloat16
    )


def prepare_plain(values, gain_vector):
    return rms_scale(values, gain_vector).astype(jnp.bfloat16)


def block_rows(overall):
    chosen = min(overall, 1024)
    while overall % chosen:
        chosen -= 1
    return chosen


def attend_one(query_rows, key_rows, value_rows, key_mask, score_scale):
    overall, head_dim = query_rows.shape
    chosen = block_rows(overall)
    grouped = query_rows.reshape(overall // chosen, chosen, head_dim)

    def one_block(rows_block):
        scores = (
            jnp.einsum("qd,kd->qk", rows_block, key_rows, preferred_element_type=jnp.float32)
            * score_scale
        )
        weights = jnp.exp(scores) * key_mask[None, :]
        denominator = jnp.sum(weights, axis=-1, keepdims=True)
        summed = jnp.dot(
            weights.astype(jnp.bfloat16), value_rows, preferred_element_type=jnp.float32
        )
        return (summed / denominator).astype(jnp.bfloat16)

    return lax.map(one_block, grouped).reshape(overall, head_dim)


def advance(attended, stream, weight_heads, gate_rows):
    projected = jnp.einsum(
        "bhrd,hde->bre", attended, weight_heads, preferred_element_type=jnp.float32
    )
    return stream.astype(jnp.float32) + gate_rows[:, None, :] * projected


def body(
    video_query,
    video_key,
    video_value,
    text_query,
    text_key,
    text_value,
    positions,
    text_lengths,
    query_gain,
    key_gain,
    out_weight,
    branch_gates,
    video_stream,
    text_stream,
):
    head_count = video_query.shape[1]
    head_dim = video_query.shape[3]
    text_rows = text_query.shape[2]
    devices_sp = lax.axis_size("sp")
    item_count = 2 * head_count
    per_device = item_count // devices_sp
    score_scale = head_dim ** (-0.5)
    sp_index = lax.axis_index("sp")
    late_tables = None
    cosine_table, sine_table = rope_tables(positions, head_dim)
    video_query_ready = prepare_rotated(video_query, query_gain, cosine_table, sine_table)
    video_key_ready = prepare_rotated(video_key, key_gain, cosine_table, sine_table)
    text_query_ready = prepare_plain(text_query, query_gain)
    text_key_ready = prepare_plain(text_key, key_gain)

    def to_items(tensor):
        return tensor.reshape((item_count,) + tensor.shape[2:])

    video_queries, text_queries = (
        lax.all_to_all(
            for_sending(to_items(video_query_ready)), "sp", split_axis=0, concat_axis=1, tiled=True
        ),
        lax.all_to_all(
            for_sending(to_items(text_query_ready)), "sp", split_axis=0, concat_axis=1, tiled=True
        ),
    )
    video_keys, video_values, text_keys, text_values = (
        lax.all_to_all(
            for_sending(to_items(video_key_ready)), "sp", split_axis=0, concat_axis=1, tiled=True
        ),
        lax.all_to_all(
            for_sending(to_items(video_value)), "sp", split_axis=0, concat_axis=1, tiled=True
        ),
        lax.all_to_all(
            for_sending(to_items(text_key_ready)), "sp", split_axis=0, concat_axis=1, tiled=True
        ),
        lax.all_to_all(
            for_sending(to_items(text_value)), "sp", split_axis=0, concat_axis=1, tiled=True
        ),
    )
    item_index = sp_index * per_device + jnp.arange(per_device, dtype=jnp.int32)
    limits = jnp.where(item_index // head_count == 0, text_lengths[0], text_lengths[1])
    text_mask = (
        jnp.arange(text_rows * devices_sp, dtype=jnp.int32)[None, :] < limits[:, None]
    ).astype(jnp.float32)
    attend_video_queries = video_queries
    attend_video_keys = video_keys
    attend_text_queries = text_queries
    attend_text_keys = text_keys
    if late_tables is not None:
        attend_video_queries = prepare_rotated(
            attend_video_queries, query_gain, late_tables[0], late_tables[1]
        )
        attend_video_keys = prepare_rotated(
            attend_video_keys, key_gain, late_tables[0], late_tables[1]
        )
        attend_text_queries = prepare_plain(attend_text_queries, query_gain)
        attend_text_keys = prepare_plain(attend_text_keys, key_gain)
    video_span = attend_video_queries.shape[1]
    queries = jnp.concatenate([attend_video_queries, attend_text_queries], axis=1)
    key_rows = jnp.concatenate([attend_video_keys, attend_text_keys], axis=1)
    value_rows = jnp.concatenate([video_values, text_values], axis=1)
    masks = jnp.concatenate(
        [jnp.ones((text_mask.shape[0], video_span), jnp.float32), text_mask], axis=1
    )

    def attend_packed(packed):
        return attend_one(packed[0], packed[1], packed[2], packed[3], score_scale)

    attended = lax.map(attend_packed, (queries, key_rows, value_rows, masks))
    video_out = attended[:, :video_span]
    text_out = attended[:, video_span:]
    video_home, text_home = (
        lax.all_to_all(
            for_sending(video_out), "sp", split_axis=1, concat_axis=0, tiled=True
        ).astype(video_out.dtype),
        lax.all_to_all(for_sending(text_out), "sp", split_axis=1, concat_axis=0, tiled=True).astype(
            text_out.dtype
        ),
    )
    video_home = video_home.reshape((2, head_count) + video_home.shape[1:])
    text_home = text_home.reshape((2, head_count) + text_home.shape[1:])
    weight_heads = out_weight.reshape(head_count, head_dim, out_weight.shape[1])
    video_streams = advance(video_home, video_stream, weight_heads, branch_gates)
    text_streams = advance(text_home, text_stream, weight_heads, branch_gates)
    guided = (video_streams[1] + guidance_scale * (video_streams[0] - video_streams[1])).astype(
        jnp.bfloat16
    )
    return (guided, video_streams.astype(jnp.bfloat16), text_streams.astype(jnp.bfloat16))


def solution(mesh):
    return jax.shard_map(
        body,
        mesh=mesh,
        in_specs=(
            P("grp", None, "sp", None),
            P("grp", None, "sp", None),
            P("grp", None, "sp", None),
            P("grp", None, "sp", None),
            P("grp", None, "sp", None),
            P("grp", None, "sp", None),
            P("grp", "sp"),
            P("grp"),
            P(),
            P(),
            P(),
            P("grp", None),
            P("grp", "sp", None),
            P("grp", "sp", None),
        ),
        out_specs=(P("sp", "grp"), P("grp", "sp", None), P("grp", "sp", None)),
        check_vma=False,
    )
```

profile of v0, /device:TPU:11, one launch (start us, length us, event | category | flops | bytes accessed | tf_op | source)
XLA Modules:
  0.0 229.4 jit_solution(76300821329885781)
XLA Ops:
  0.7 1.2 fusion.41
  1.9 1.7 fusion.43
  3.6 6.6 %all-to-all-start.3 = ((bf16[32,16,128]{2,1,0:T(8,128)(2,1)}), bf16[32,16,128]{2,1,0:T(8,128)(2,1)S(1)}, u32[]{:S(2)}, u32[]{:S(2)}) async-start(bf16[32,16,128]{2,1,0:T(8,128)(2,1)} %bitcast.21), calls=%async_computation.3 | async-start | bytes 262144 | tf_op jit(solution)/shard_map/all_to_all | solution.py:146
  10.2 1.8 fusion.22
  12.0 0.6 fusion.24
  12.7 0.7 fusion.23
  13.4 2.7 %fusion.55 = (f32[2,16,128,1]{3,2,1,0:T(8,128)}, f32[2,16,128,1]{3,2,1,0:T(8,128)}) fusion(f32[2,16,128,128]{3,2,1,0:T(8,128)S(1)} %fusion.23), kind=kLoop, calls=%fused_computation.103 | loop fusion | bytes 65536 | tf_op jit(solution)/shard_map/jit(_roll_static)/slice | solution.py:49
  16.1 2.8 %fusion.56 = (f32[2,16,128,127]{3,2,1,0:T(8,128)}, f32[2,16,128,127]{3,2,1,0:T(8,128)}) fusion(f32[2,16,128,128]{3,2,1,0:T(8,128)S(1)} %fusion.23), kind=kLoop, calls=%fused_computation.104 | loop fusion | bytes 8323072 | tf_op jit(solution)/shard_map/jit(_roll_static)/slice | solution.py:49
  18.9 0.7 fusion.25
  19.5 2.7 %fusion.53 = (f32[2,16,128,1]{3,2,1,0:T(8,128)}, f32[2,16,128,1]{3,2,1,0:T(8,128)}) fusion(f32[2,16,128,128]{3,2,1,0:T(8,128)S(1)} %fusion.25), kind=kLoop, calls=%fused_computation.101 | loop fusion | bytes 65536 | tf_op jit(solution)/shard_map/jit(_roll_static)/slice | solution.py:49
  22.2 2.8 %fusion.54 = (f32[2,16,128,127]{3,2,1,0:T(8,128)}, f32[2,16,128,127]{3,2,1,0:T(8,128)}) fusion(f32[2,16,128,128]{3,2,1,0:T(8,128)S(1)} %fusion.25), kind=kLoop, calls=%fused_computation.102 | loop fusion | bytes 8323072 | tf_op jit(solution)/shard_map/jit(_roll_static)/slice | solution.py:49
  25.2 0.8 fusion.40
  26.0 6.0 %all-to-all-start.1 = ((bf16[32,16,128]{2,1,0:T(8,128)(2,1)}), bf16[32,16,128]{2,1,0:T(8,128)(2,1)S(1)}, u32[]{:S(2)}, u32[]{:S(2)}) async-start(bf16[32,16,128]{2,1,0:T(8,128)(2,1)} %bitcast.13), calls=%async_computation.1 | async-start | bytes 262144 | tf_op jit(solution)/shard_map/all_to_all | solution.py:135
  32.0 0.5 fusion.48
  32.5 1.0 fusion.45
  33.5 4.4 %all-to-all-done.1 = bf16[32,16,128]{2,1,0:T(8,128)(2,1)S(1)} async-done(((bf16[32,16,128]{2,1,0:T(8,128)(2,1)}), bf16[32,16,128]{2,1,0:T(8,128)(2,1)S(1)}, u32[]{:S(2)}, u32[]{:S(2)}) %all-to-all-start.1) | async-done | bytes 131104 | tf_op jit(solution)/shard_map/all_to_all | solution.py:135
  37.9 5.4 %all-to-all-start.5 = ((bf16[32,16,128]{2,1,0:T(8,128)(2,1)}), bf16[32,16,128]{2,1,0:T(8,128)(2,1)S(1)}, u32[]{:S(2)}, u32[]{:S(2)}) async-start(bf16[32,16,128]{2,1,0:T(8,128)(2,1)} %bitcast.31), calls=%async_computation.5 | async-start | bytes 262144 | tf_op jit(solution)/shard_map/all_to_all | solution.py:149
  43.3 8.5 %fusion.33 = (bf16[2,16,128,128]{3,2,1,0:T(8,128)(2,1)}, bf16[2,16,128,128]{3,2,1,0:T(8,128)(2,1)S(1)}) fusion(f32[2,16,128,1]{3,2,1,0:T(8,128)} %get-tuple-element.97, f32[2,16,128,127]{3,2,1,0:T(8,128)} %get-tuple-element.99, f32[2,16,128,127]{3,2,1,0:T(8,128)} %get-tuple-element.98, f32[2,16,128,1]{3,2,1,0:T(8,128)} %get-tuple-element.96, ...), kind=kLoop, calls=%fused_computation.39 | loop fusion | flops 11534336 | bytes 12747904 | tf_op jit(solution)/shard_map/convert_element_type | solution.py:54
  51.8 31.4 %all_to_all.138 = bf16[32,128,128]{2,1,0:T(8,128)(2,1)S(1)} all-to-all(bf16[32,128,128]{2,1,0:T(8,128)(2,1)} %bitcast.124), channel_id=1, replica_groups=mesh['grp'=2,'sp'=16] {'sp'}, dimensions={0} | all-to-all | bytes 2097152 | tf_op jit(solution)/shard_map/all_to_all | solution.py:140
  83.2 29.7 %all_to_all.139 = bf16[32,128,128]{2,1,0:T(8,128)(2,1)} all-to-all(bf16[32,128,128]{2,1,0:T(8,128)(2,1)S(1)} %bitcast.123), channel_id=1, replica_groups=mesh['grp'=2,'sp'=16] {'sp'}, dimensions={0} | all-to-all | bytes 2097152 | tf_op jit(solution)/shard_map/all_to_all | solution.py:132
  113.0 4.5 %all-to-all-start.4 = ((bf16[32,128,128]{2,1,0:T(8,128)(2,1)}), bf16[32,128,128]{2,1,0:T(8,128)(2,1)S(1)}, u32[]{:S(2)}, u32[]{:S(2)}) async-start(bf16[32,128,128]{2,1,0:T(8,128)(2,1)} %bitcast.132), calls=%async_computation.4 | async-start | bytes 2097152 | tf_op jit(solution)/shard_map/all_to_all | solution.py:143
  117.5 0.6 fusion.57
  118.1 1.2 compare_select_fusion
  119.5 0.6 pad_convert_fusion
  120.1 0.9 copy.30
  121.0 0.9 copy.34
  121.9 1.0 copy.31
  123.0 1.1 copy.29
  124.1 18.3 %all-to-all-done.4 = bf16[32,128,128]{2,1,0:T(8,128)(2,1)S(1)} async-done(((bf16[32,128,128]{2,1,0:T(8,128)(2,1)}), bf16[32,128,128]{2,1,0:T(8,128)(2,1)S(1)}, u32[]{:S(2)}, u32[]{:S(2)}) %all-to-all-start.4) | async-done | bytes 1048608 | tf_op jit(solution)/shard_map/all_to_all | solution.py:143
  142.6 1.0 copy-done.4
  143.6 1.1 pad_maximum_fusion
  144.8 1.1 pad_maximum_fusion.2
  145.9 23.4 %while.21 = (s32[]{:T(128)}, bf16[2,2304,128]{2,1,0:T(8,128)(2,1)}, bf16[2,2304,128]{2,1,0:T(8,128)(2,1)}, bf16[2,2304,128]{2,1,0:T(8,128)(2,1)S(1)}, f32[2,2304...) while((s32[]{:T(128)}, bf16[2,2304,128]{2,1,0:T(8,128)(2,1)}, ...), condition=%wide.region_8.9_spmd, body=%wide.region_4.8_spmd.sunk | while | flops 913243392 | bytes 18126616 | solution.py:182
  145.9 1.2 dynamic-slice_bitcast_fusion.3
  147.3 0.8 dynamic-slice_reduce_fusion.2
  148.1 8.6 %while.22 = (s32[]{:T(128)}, bf16[3,768,128]{2,1,0:T(8,128)(2,1)S(1)}, bf16[3,768,128]{2,1,0:T(8,128)(2,1)S(1)}, bf16[2304,128]{1,0:T(8,128)(2,1)S(1)}, f32[2304...) while((s32[]{:T(128)}, bf16[3,768,128]{2,1,0:T(8,128)(2,1)S(1)}, ...), condition=%wide.region_7.7_spmd, body=%wide.region_5.6_spmd.sunk | while | flops 913243392 | bytes 8670293 | solution.py:87
  148.1 1.7 fusion.74
  149.8 1.2 fusion.75
  151.0 1.7 fusion.74
  152.6 1.2 fusion.75
  153.8 1.7 fusion.74
  155.5 1.2 fusion.75
  156.7 0.9 bitcast_dynamic-update-slice_fusion.2
  157.5 1.2 dynamic-slice_bitcast_fusion.3
  159.0 0.8 dynamic-slice_reduce_fusion.2
  159.8 8.6 %while.22 = (s32[]{:T(128)}, bf16[3,768,128]{2,1,0:T(8,128)(2,1)S(1)}, bf16[3,768,128]{2,1,0:T(8,128)(2,1)S(1)}, bf16[2304,128]{1,0:T(8,128)(2,1)S(1)}, f32[2304...) while((s32[]{:T(128)}, bf16[3,768,128]{2,1,0:T(8,128)(2,1)S(1)}, ...), condition=%wide.region_7.7_spmd, body=%wide.region_5.6_spmd.sunk | while | flops 913243392 | bytes 8670293 | solution.py:87
  159.8 1.7 fusion.74
  161.5 1.2 fusion.75
  162.7 1.7 fusion.74
  164.3 1.2 fusion.75
  165.5 1.7 fusion.74
  167.2 1.2 fusion.75
  168.4 0.9 bitcast_dynamic-update-slice_fusion.2
  169.2 9.6 %copy.35 = bf16[2,2304,128]{2,0,1:T(2,128)(2,1)S(1)} copy(bf16[2,2304,128]{2,1,0:T(8,128)(2,1)} %get-tuple-element.67) | data formatting | bytes 2359296 | tf_op jit(solution)/shard_map/while | solution.py:182
  178.8 0.7 slice.84
  179.5 4.8 %all-to-all-start.7 = ((bf16[2,256,128]{2,0,1:T(2,128)(2,1)}), bf16[2,256,128]{2,0,1:T(2,128)(2,1)S(1)}, u32[]{:S(2)}, u32[]{:S(2)}) async-start(bf16[2,256,128]{2,0,1:T(2,128)(2,1)} %slice.84), calls=%async_computation.7 | async-start | bytes 262144 | tf_op jit(solution)/shard_map/all_to_all | solution.py:189
  184.3 1.6 slice.81
  185.9 4.3 %all-to-all-done.7 = bf16[2,256,128]{2,0,1:T(2,128)(2,1)S(1)} async-done(((bf16[2,256,128]{2,0,1:T(2,128)(2,1)}), bf16[2,256,128]{2,0,1:T(2,128)(2,1)S(1)}, u32[]{:S(2)}, u32[]{:S(2)}) %all-to-all-start.7) | async-done | bytes 131104 | tf_op jit(solution)/shard_map/all_to_all | solution.py:189
  190.2 5.6 %all-to-all-start.6 = ((bf16[2,2048,128]{2,0,1:T(2,128)(2,1)}), bf16[2,2048,128]{2,0,1:T(2,128)(2,1)S(1)}, u32[]{:S(2)}, u32[]{:S(2)}) async-start(bf16[2,2048,128]{2,0,1:T(2,128)(2,1)} %slice.81), calls=%async_computation.6 | async-start | bytes 2097152 | tf_op jit(solution)/shard_map/all_to_all | solution.py:186
  195.8 6.5 %fusion.21 = bf16[2,16,3072]{2,1,0:T(8,128)(2,1)} fusion(bf16[2,16,16,128]{3,2,1,0:T(8,128)(2,1)S(1)} %bitcast.134, bf16[16,128,3072,1]{2,1,0,3:T(8,128)(2,1)} %bitcast.119, bf16[2,16,3072]{2,1,0:T(8,128)(2,1)S(1)} %copy-done.9, f32[2,3072]{1,0:T(2,128)S(1)} %copy-done.11), kind=kOutput, calls=%fused_computation.21 | convolution fusion | flops 403046400 | bytes 13131776 | tf_op jit(solution)/shard_map/bhrd,hde->bre/dot_general | solution.py:91
  202.3 18.4 %all-to-all-done.6 = bf16[2,2048,128]{2,0,1:T(2,128)(2,1)S(1)} async-done(((bf16[2,2048,128]{2,0,1:T(2,128)(2,1)}), bf16[2,2048,128]{2,0,1:T(2,128)(2,1)S(1)}, u32[]{:S(2)}, u32[]{:S(2)}) %all-to-all-start.6) | async-done | bytes 1048608 | tf_op jit(solution)/shard_map/all_to_all | solution.py:186
  220.7 0.2 copy.36
  221.0 7.4 %fusion.58 = (bf16[2,128,3072]{2,1,0:T(8,128)(2,1)}, f32[2,128,3072]{2,1,0:T(8,128)S(1)}) fusion(bf16[2,16,128,128]{3,2,1,0:T(8,128)(2,1)S(1)} %bitcast.133, bf16[16,128,3072,1]{2,1,0,3:T(8,128)(2,1)} %bitcast.120, f32[2,3072]{1,0:T(2,128)S(1)} %copy-done.11, bf16[2,128,3072]{2,1,0:T(8,128)(2,1)S(1)} %copy-done.16), kind=kOutput, calls=%fused_computation.106 | convolution fusion | flops 3224371200 | bytes 19947520 | tf_op jit(solution)/shard_map/bhrd,hde->bre/dot_general | solution.py:91
  228.3 1.1 fusion.37
  (54 shorter events, 1.0 us)
Async XLA Ops:
  0.6 11.4 %copy-start.1 = (bf16[2,16,128,128]{3,2,1,0:T(8,128)(2,1)S(1)}, bf16[2,16,128,128]{3,2,1,0:T(8,128)(2,1)}, u32[]{:S(2)}) copy-start(bf16[2,16,128,128]{3,2,1,0:T(8,128)(2,1)} %param.19) | copy-start | bytes 3145732
  0.6 12.0 %copy-start.2 = (bf16[2,16,128,128]{3,2,1,0:T(8,128)(2,1)S(1)}, bf16[2,16,128,128]{3,2,1,0:T(8,128)(2,1)}, u32[]{:S(2)}) copy-start(bf16[2,16,128,128]{3,2,1,0:T(8,128)(2,1)} %param.18) | copy-start | bytes 3145732
  0.7 12.0 %copy-start.12 = (f32[128]{0:T(128)S(1)}, f32[128]{0:T(128)}, u32[]{:S(2)}) copy-start(f32[128]{0:T(128)} %param.26) | copy-start | bytes 1540
  3.6 22.4 %all-to-all-start.3 = ((bf16[32,16,128]{2,1,0:T(8,128)(2,1)}), bf16[32,16,128]{2,1,0:T(8,128)(2,1)S(1)}, u32[]{:S(2)}, u32[]{:S(2)}) async-start(bf16[32,16,128]{2,1,0:T(8,128)(2,1)} %bitcast.21), calls=%async_computation.3 | async-start | bytes 262144 | tf_op jit(solution)/shard_map/all_to_all | solution.py:146
  12.7 3.4 %copy-start.10 = (f32[2,16,128]{2,1,0:T(8,128)}, f32[2,16,128]{2,1,0:T(8,128)S(1)}, u32[]{:S(2)}) copy-start(f32[2,16,128]{2,1,0:T(8,128)S(1)} %get-tuple-element.118) | copy-start | bytes 49156
  16.1 2.8 %copy-start.13 = (f32[128]{0:T(128)S(1)}, f32[128]{0:T(128)}, u32[]{:S(2)}) copy-start(f32[128]{0:T(128)} %param.27) | copy-start | bytes 1540
  22.2 2.8 %copy-start.15 = (s32[3,128]{1,0:T(4,128)S(1)}, s32[3,128]{1,0:T(4,128)}, u32[]{:S(2)}) copy-start(s32[3,128]{1,0:T(4,128)} %param.24) | copy-start | bytes 4612
  22.2 2.8 %copy-start.6 = (bf16[2,16,16,128]{3,2,1,0:T(8,128)(2,1)S(1)}, bf16[2,16,16,128]{3,2,1,0:T(8,128)(2,1)}, u32[]{:S(2)}) copy-start(bf16[2,16,16,128]{3,2,1,0:T(8,128)(2,1)} %param.21) | copy-start | bytes 393220
  26.0 11.9 %all-to-all-start.1 = ((bf16[32,16,128]{2,1,0:T(8,128)(2,1)}), bf16[32,16,128]{2,1,0:T(8,128)(2,1)S(1)}, u32[]{:S(2)}, u32[]{:S(2)}) async-start(bf16[32,16,128]{2,1,0:T(8,128)(2,1)} %bitcast.13), calls=%async_computation.1 | async-start | bytes 262144 | tf_op jit(solution)/shard_map/all_to_all | solution.py:135
  37.9 13.9 %copy-start.7 = (bf16[32,16,128]{2,1,0:T(8,128)(2,1)}, bf16[32,16,128]{2,1,0:T(8,128)(2,1)S(1)}, u32[]{:S(2)}) copy-start(bf16[32,16,128]{2,1,0:T(8,128)(2,1)S(1)} %all-to-all-done.1) | copy-start | bytes 393220
  37.9 13.9 %all-to-all-start.5 = ((bf16[32,16,128]{2,1,0:T(8,128)(2,1)}), bf16[32,16,128]{2,1,0:T(8,128)(2,1)S(1)}, u32[]{:S(2)}, u32[]{:S(2)}) async-start(bf16[32,16,128]{2,1,0:T(8,128)(2,1)} %bitcast.31), calls=%async_computation.5 | async-start | bytes 262144 | tf_op jit(solution)/shard_map/all_to_all | solution.py:149
  51.8 61.2 %copy-start.8 = (bf16[32,16,128]{2,1,0:T(8,128)(2,1)}, bf16[32,16,128]{2,1,0:T(8,128)(2,1)S(1)}, u32[]{:S(2)}) copy-start(bf16[32,16,128]{2,1,0:T(8,128)(2,1)S(1)} %all-to-all-done.5) | copy-start | bytes 393220
  83.2 34.2 %copy-start.14 = (s32[2]{0:T(128)S(1)}, s32[2]{0:T(128)}, u32[]{:S(2)}) copy-start(s32[2]{0:T(128)} %param.25) | copy-start | bytes 28
  113.0 10.0 %copy-start.3 = (bf16[32,128,128]{2,1,0:T(8,128)(2,1)S(1)}, bf16[32,128,128]{2,1,0:T(8,128)(2,1)}, u32[]{:S(2)}) copy-start(bf16[32,128,128]{2,1,0:T(8,128)(2,1)} %all_to_all.139) | copy-start | bytes 3145732
  113.0 29.4 %all-to-all-start.4 = ((bf16[32,128,128]{2,1,0:T(8,128)(2,1)}), bf16[32,128,128]{2,1,0:T(8,128)(2,1)S(1)}, u32[]{:S(2)}, u32[]{:S(2)}) async-start(bf16[32,128,128]{2,1,0:T(8,128)(2,1)} %bitcast.132), calls=%async_computation.4 | async-start | bytes 2097152 | tf_op jit(solution)/shard_map/all_to_all | solution.py:143
  124.1 18.4 %copy-start.5 = (bf16[2,16,128,128]{3,2,1,0:T(8,128)(2,1)S(1)}, bf16[2,16,128,128]{3,2,1,0:T(8,128)(2,1)}, u32[]{:S(2)}) copy-start(bf16[2,16,128,128]{3,2,1,0:T(8,128)(2,1)} %copy.31) | copy-start | bytes 3145732
  142.4 1.2 copy-start.4
  145.9 1.4 copy-start
  157.5 1.4 copy-start
  179.5 10.7 %all-to-all-start.7 = ((bf16[2,256,128]{2,0,1:T(2,128)(2,1)}), bf16[2,256,128]{2,0,1:T(2,128)(2,1)S(1)}, u32[]{:S(2)}, u32[]{:S(2)}) async-start(bf16[2,256,128]{2,0,1:T(2,128)(2,1)} %slice.84), calls=%async_computation.7 | async-start | bytes 262144 | tf_op jit(solution)/shard_map/all_to_all | solution.py:189
  184.3 11.5 %copy-start.9 = (bf16[2,16,3072]{2,1,0:T(8,128)(2,1)S(1)}, bf16[2,16,3072]{2,1,0:T(8,128)(2,1)}, u32[]{:S(2)}) copy-start(bf16[2,16,3072]{2,1,0:T(8,128)(2,1)} %param.31) | copy-start | bytes 589828
  184.3 11.5 %copy-start.11 = (f32[2,3072]{1,0:T(2,128)S(1)}, f32[2,3072]{1,0:T(2,128)}, u32[]{:S(2)}) copy-start(f32[2,3072]{1,0:T(2,128)} %param.29) | copy-start | bytes 73732
  190.2 30.5 %all-to-all-start.6 = ((bf16[2,2048,128]{2,0,1:T(2,128)(2,1)}), bf16[2,2048,128]{2,0,1:T(2,128)(2,1)S(1)}, u32[]{:S(2)}, u32[]{:S(2)}) async-start(bf16[2,2048,128]{2,0,1:T(2,128)(2,1)} %slice.81), calls=%async_computation.6 | async-start | bytes 2097152 | tf_op jit(solution)/shard_map/all_to_all | solution.py:186
  202.3 18.6 %copy-start.16 = (bf16[2,128,3072]{2,1,0:T(8,128)(2,1)S(1)}, bf16[2,128,3072]{2,1,0:T(8,128)(2,1)}, u32[]{:S(2)}) copy-start(bf16[2,128,3072]{2,1,0:T(8,128)(2,1)} %param.30) | copy-start | bytes 4718596
where the time goes:
time: 231 us; the launch traced here: 229 us
  blocking collectives  61.2 us (26%)
  waiting for transfers between devices  45.4 us (20%)
  local copies, waits for them, and re-layouts  35 us (15%)
  starting transfers between devices  32.9 us (14%)
  matrix products  30.9 us (13%)
  other arithmetic  23 us (10%)
    all_to_all x1, blocking collectives, body(): lax.all_to_all(for_sending(to_items(video_key_ready)), 'sp', split_axis=0...  31.4 us
    all_to_all x1, blocking collectives, body(): lax.all_to_all(for_sending(to_items(video_query_ready)), 'sp', split_axis...  29.7 us
    all_to_all x1, waiting for transfers between devices, body(): lax.all_to_all(for_sending(video_out), 'sp', split_axis=1, concat_axis=0,...  18.4 us
    all_to_all x1, waiting for transfers between devices, body(): lax.all_to_all(for_sending(to_items(video_value)), 'sp', split_axis=0, co...  18.3 us
    dot_general x2, matrix products, advance(): jnp.einsum('bhrd,hde->bre', attended, weight_heads, preferred_element_typ...  13.9 us
    slice x4, local copies, waits for them, and re-layouts, rotate_pairs(): jnp.roll(values, 1, axis=-1)  10.9 us
    dot_general x6, matrix products, one_block(): jnp.einsum('qd,kd->qk', rows_block, key_rows, preferred_element_type=jnp....  10 us
    while x1, local copies, waits for them, and re-layouts, body(): attended = lax.map(attend_packed, (queries, key_rows, value_rows, masks))  9.55 us
  transfers between devices with their start and end apart: 6, of which 4 were waited for; matrix products, arithmetic and copies ran while one was open for 18% of the time, Pallas kernels for 0%

commit v1 on v0

v1 whole, which is shorter than its diff:
```python
import functools
import math

import jax
import jax.numpy as jnp
from jax import lax
from jax.experimental import pallas as pl
from jax.experimental.pallas import tpu as pltpu
from jax.sharding import PartitionSpec as P

norm_eps = 1e-06
rope_theta = 256.0
guidance_scale = 5.0

MESH = pl.DeviceIdType.MESH
F32 = jnp.float32
BF16 = jnp.bfloat16
V, K, Q, O = 0, 1, 2, 3


def swapped(rows):
    even = lax.broadcasted_iota(jnp.int32, rows.shape, 1) % 2 == 0
    last = rows.shape[1] - 1
    return jnp.where(even, pltpu.roll(rows, last, 1), pltpu.roll(rows, 1, 1))


def rope_tables(positions, head_dim):
    frame_width = head_dim // 8
    side_width = 7 * head_dim // 16
    starts = (0, frame_width, frame_width + side_width)
    extents = (frame_width, side_width, side_width)
    tokens = positions.shape[1]
    channel = lax.broadcasted_iota(jnp.int32, (head_dim, tokens), 0)
    angles = jnp.zeros((head_dim, tokens), F32)
    for slot in range(3):
        inside = (channel >= starts[slot]) & (channel < starts[slot] + extents[slot])
        within = ((channel - starts[slot]) // 2).astype(F32)
        frequency = jnp.where(
            inside, jnp.exp(-2.0 * within / extents[slot] * math.log(rope_theta)), 0.0
        )
        angles = angles + positions[slot : slot + 1, :].astype(F32) * frequency
    return jnp.cos(angles).T, jnp.sin(angles).T


def kernel(
    n,
    heads,
    chunk,
    group,
    vq_ref,
    vk_ref,
    vv_ref,
    tq_ref,
    tk_ref,
    tv_ref,
    pos_ref,
    len_ref,
    qg_ref,
    kg_ref,
    weight_hbm,
    gate_ref,
    vstream_hbm,
    tstream_hbm,
    guided_ref,
    vnext_ref,
    tnext_ref,
    comb,
    got,
    osend,
    ohome,
    vext,
    tables,
    weight,
    vstream,
    tstream,
    acc,
    send_sem,
    recv_sem,
    local_sem,
):
    me = lax.axis_index("sp")
    items, rows_v, head_dim = vq_ref.shape
    rows_t = tq_ref.shape[1]
    rows = comb.shape[2]
    waves = items // n
    width = weight.shape[1]

    barrier = pltpu.get_barrier_semaphore()

    @pl.loop(1, n)
    def _(i):
        pl.semaphore_signal(
            barrier, inc=1, device_id={"sp": lax.rem(me + i, n)}, device_id_type=MESH
        )

    loads = (
        pltpu.make_async_copy(weight_hbm, weight, local_sem.at[0]),
        pltpu.make_async_copy(vstream_hbm, vstream, local_sem.at[1]),
        pltpu.make_async_copy(tstream_hbm, tstream, local_sem.at[2]),
    )
    for load in loads:
        load.start()

    def copy_in(kind, wave, owner, target):
        return pltpu.make_async_remote_copy(
            src_ref=comb.at[kind, wave * n + target],
            dst_ref=got.at[kind, wave, owner],
            send_sem=send_sem.at[kind, wave, target],
            recv_sem=recv_sem.at[kind, wave, owner],
            device_id={"sp": target},
            device_id_type=MESH,
        )

    def copy_back(wave, owner, target):
        return pltpu.make_async_remote_copy(
            src_ref=osend.at[wave, target],
            dst_ref=ohome.at[wave * n + owner],
            send_sem=send_sem.at[O, wave, target],
            recv_sem=recv_sem.at[O, wave, owner],
            device_id={"sp": target},
            device_id_type=MESH,
        )

    def deal(kind, wave, make):
        @pl.loop(0, n)
        def _(i):
            target = lax.rem(me + i, n)
            video, text = make(wave * n + target)

            def put(ref):
                ref[pl.ds(0, rows_v), :] = video
                ref[pl.ds(rows_v, rows_t), :] = text
                if rows > rows_v + rows_t:
                    spare = rows - rows_v - rows_t
                    ref[pl.ds(rows_v + rows_t, spare), :] = jnp.zeros((spare, head_dim), BF16)

            @pl.when(target == me)
            def _():
                put(got.at[kind, wave, me])

            @pl.when(target != me)
            def _():
                put(comb.at[kind, wave * n + target])
                copy_in(kind, wave, me, target).start()

    def make_value(item):
        return vv_ref[item], tv_ref[item]

    def inverse_rms(wide):
        return lax.rsqrt(jnp.mean(wide * wide, axis=-1, keepdims=True) + norm_eps)

    source = lax.broadcasted_iota(jnp.int32, (head_dim, head_dim), 0)
    dest = lax.broadcasted_iota(jnp.int32, (head_dim, head_dim), 1)
    partner_of = jnp.where(
        (dest % 2 == 0) & (source == dest + 1),
        -1.0,
        jnp.where((dest % 2 == 1) & (source == dest - 1), 1.0, 0.0),
    ).astype(BF16)

    def make_normed(video_ref, text_ref, slot, gain):
        def make(item):
            raw = video_ref[item]
            wide = raw.astype(F32)
            partner = jnp.dot(raw, partner_of, preferred_element_type=F32)
            video = inverse_rms(wide) * (
                wide * tables[slot, 0] + partner * tables[slot, 1]
            )
            plain = text_ref[item].astype(F32)
            text = plain * inverse_rms(plain) * gain
            return video.astype(BF16), text.astype(BF16)

        return make

    pl.semaphore_wait(barrier, n - 1)
    deal(V, 0, make_value)

    query_gain = qg_ref[...] * (head_dim ** (-0.5) * math.log2(math.e))
    key_gain = kg_ref[...]
    cosine, sine = rope_tables(pos_ref[...], head_dim)
    for slot, gain in ((0, key_gain), (1, query_gain)):
        tall = jnp.broadcast_to(gain, (8, head_dim))
        tables[slot, 0] = cosine * gain
        tables[slot, 1] = sine * swapped(tall)[0:1, :]

    make_key = make_normed(vk_ref, tk_ref, 0, key_gain)
    make_query = make_normed(vq_ref, tq_ref, 1, query_gain)
    for wave in range(waves):
        if wave > 0:
            deal(V, wave, make_value)
        deal(K, wave, make_key)
        deal(Q, wave, make_query)

    acc[...] = jnp.zeros_like(acc)

    row = lax.broadcasted_iota(jnp.int32, (rows, 1), 0)
    for wave in range(waves):
        limit = len_ref[(wave * n + me) // heads]

        @pl.loop(0, n)
        def _(owner):
            @pl.when(owner != me)
            def _():
                copy_in(V, wave, owner, me).wait_recv()
                copy_in(K, wave, owner, me).wait_recv()

            text_index = owner * rows_t + row - rows_v
            live = (row < rows_v) | ((row < rows_v + rows_t) & (text_index < limit))
            counted = jnp.broadcast_to(jnp.where(live, 1.0, 0.0), (rows, head_dim)).astype(BF16)
            vext[owner, :, pl.ds(0, head_dim)] = got[V, wave, owner] * counted
            vext[owner, :, pl.ds(head_dim, head_dim)] = counted

        @pl.loop(0, n // chunk)
        def _(step):
            first = lax.rem(me // chunk + step, n // chunk) * chunk
            for j in range(chunk):

                @pl.when(first + j != me)
                def _():
                    copy_in(Q, wave, first + j, me).wait_recv()

            queries = got[Q, wave, pl.ds(first, chunk)].reshape(chunk * rows, head_dim)
            keys = got[K, wave].reshape(n * rows, head_dim)
            scores = lax.dot_general(
                queries, keys, (((1,), (1,)), ((), ())), preferred_element_type=F32
            )
            weights = jnp.exp2(scores).astype(BF16)
            summed = jnp.dot(
                weights, vext[...].reshape(n * rows, 2 * head_dim), preferred_element_type=F32
            )
            attended = (summed[:, :head_dim] / summed[:, head_dim:]).astype(BF16)
            for j in range(chunk):
                part = attended[j * rows : (j + 1) * rows]

                @pl.when(first + j == me)
                def _():
                    ohome[wave * n + me] = part

                @pl.when(first + j != me)
                def _():
                    osend[wave, first + j] = part
                    copy_back(wave, me, first + j).start()

    loads[0].wait()
    tile = math.gcd(width, 768)
    for wave in range(waves):

        @pl.loop(0, n // group)
        def _(step):
            first = lax.rem(me // group + n // group - step, n // group) * group
            for j in range(group):

                @pl.when(first + j != me)
                def _():
                    copy_back(wave, first + j, me).wait_recv()

            item = wave * n + first
            branch, head = item // heads, lax.rem(item, heads)
            rows_in = jnp.concatenate([ohome[item + j] for j in range(group)], axis=1)

            @pl.loop(0, width // tile)
            def _(t):
                columns = pl.ds(pl.multiple_of(t * tile, tile), tile)
                depth = pl.ds(pl.multiple_of(head * head_dim, head_dim), group * head_dim)
                acc[branch, :, columns] += jnp.dot(
                    rows_in, weight[depth, columns], preferred_element_type=F32
                )

    loads[1].wait()
    loads[2].wait()

    @pl.loop(0, width // tile)
    def _(t):
        columns = pl.ds(pl.multiple_of(t * tile, tile), tile)
        streams = []
        for branch in range(2):
            gate = gate_ref[pl.ds(branch, 1), columns]
            stream = vstream[branch, :, columns].astype(F32) + gate * acc[
                branch, pl.ds(0, rows_v), columns
            ]
            vnext_ref[branch, :, columns] = stream.astype(BF16)
            streams.append(stream)
            tnext_ref[branch, :, columns] = (
                tstream[branch, :, columns].astype(F32)
                + gate * acc[branch, pl.ds(rows_v, rows_t), columns]
            ).astype(BF16)
        guided_ref[:, columns] = (
            streams[1] + guidance_scale * (streams[0] - streams[1])
        ).astype(BF16)

    for wave in range(waves):

        @pl.loop(1, n)
        def _(i):
            target = lax.rem(me + i, n)
            for kind in (V, K, Q):
                copy_in(kind, wave, me, target).wait_send()
            copy_back(wave, me, target).wait_send()


def body(
    n,
    video_query,
    video_key,
    video_value,
    text_query,
    text_key,
    text_value,
    positions,
    text_lengths,
    query_gain,
    key_gain,
    out_weight,
    branch_gates,
    video_stream,
    text_stream,
):
    branches, heads, rows_v, head_dim = video_query.shape
    rows_t = text_query.shape[2]
    items = branches * heads
    waves = items // n
    rows = -(-(rows_v + rows_t) // 16) * 16
    width = out_weight.shape[1]
    chunk = 2 if n % 2 == 0 else 1
    group = math.gcd(math.gcd(n, heads), 4)

    def flat(tensor):
        return tensor.reshape((items,) + tensor.shape[2:])

    vmem = pl.BlockSpec(memory_space=pltpu.VMEM)
    smem = pl.BlockSpec(memory_space=pltpu.SMEM)
    anywhere = pl.BlockSpec(memory_space=pl.ANY)
    return pl.pallas_call(
        functools.partial(kernel, n, heads, chunk, group),
        out_shape=(
            jax.ShapeDtypeStruct((rows_v, width), BF16),
            jax.ShapeDtypeStruct((branches, rows_v, width), BF16),
            jax.ShapeDtypeStruct((branches, rows_t, width), BF16),
        ),
        in_specs=[vmem] * 7 + [smem, vmem, vmem, anywhere, vmem, anywhere, anywhere],
        out_specs=(vmem, vmem, vmem),
        scratch_shapes=[
            pltpu.VMEM((3, items, rows, head_dim), BF16),
            pltpu.VMEM((3, waves, n, rows, head_dim), BF16),
            pltpu.VMEM((waves, n, rows, head_dim), BF16),
            pltpu.VMEM((items, rows, head_dim), BF16),
            pltpu.VMEM((n, rows, 2 * head_dim), BF16),
            pltpu.VMEM((2, 2, rows_v, head_dim), F32),
            pltpu.VMEM(out_weight.shape, BF16),
            pltpu.VMEM(video_stream.shape, BF16),
            pltpu.VMEM(text_stream.shape, BF16),
            pltpu.VMEM((branches, rows, width), F32),
            pltpu.SemaphoreType.DMA((4, waves, n)),
            pltpu.SemaphoreType.DMA((4, waves, n)),
            pltpu.SemaphoreType.DMA((3,)),
        ],
        compiler_params=pltpu.CompilerParams(
            collective_id=0, has_side_effects=True, vmem_limit_bytes=63 * 1024 * 1024
        ),
    )(
        flat(video_query),
        flat(video_key),
        flat(video_value),
        flat(text_query),
        flat(text_key),
        flat(text_value),
        positions,
        text_lengths,
        query_gain.reshape(1, head_dim),
        key_gain.reshape(1, head_dim),
        out_weight,
        branch_gates,
        video_stream,
        text_stream,
    )


def solution(mesh):
    return jax.shard_map(
        functools.partial(body, mesh.shape["sp"]),
        mesh=mesh,
        in_specs=(
            P("grp", None, "sp", None),
            P("grp", None, "sp", None),
            P("grp", None, "sp", None),
            P("grp", None, "sp", None),
            P("grp", None, "sp", None),
            P("grp", None, "sp", None),
            P("grp", "sp"),
            P("grp"),
            P(),
            P(),
            P(),
            P("grp", None),
            P("grp", "sp", None),
            P("grp", "sp", None),
        ),
        out_specs=(P("sp", "grp"), P("grp", "sp", None), P("grp", "sp", None)),
        check_vma=False,
    )
```

time: 231 us -> 121 us (0.52)
  Pallas kernels: 0 us -> 114 us
  blocking collectives: 61.2 us -> 0 us
  waiting for transfers between devices: 45.4 us -> 0 us
  starting transfers between devices: 32.9 us -> 0 us
  local copies, waits for them, and re-layouts: 35 us -> 4.01 us
  matrix products: 30.9 us -> 0 us
  other arithmetic: 23 us -> 0 us
    pallas_call x0 -> x1, Pallas kernels: none -> 114 us  [body(): pl.pallas_call(functools.partial(kernel, n, heads, chunk, group), out_sha...]
    all_to_all x2 -> x0, blocking collectives: 61.2 us -> none  [the longest x1 31.4 us: body(): lax.all_to_all(for_sending(to_items(video_key_ready)), 'sp', split_axis=0...]
    all_to_all x6 -> x0, waiting for transfers between devices: 45.4 us -> none  [the longest x1 18.4 us: body(): lax.all_to_all(for_sending(video_out), 'sp', split_axis=1, concat_axis=0,...]
    all_to_all x6 -> x0, starting transfers between devices: 32.9 us -> none  [the longest x1 6.58 us: body(): lax.all_to_all(for_sending(to_items(text_key_ready)), 'sp', split_axis=0,...]
    dot_general x14 -> x0, matrix products: 30.9 us -> none  [the longest x2 13.9 us: advance(): jnp.einsum('bhrd,hde->bre', attended, weight_heads, preferred_element_typ...]
    slice x7 -> x0, local copies, waits for them, and re-layouts: 13.8 us -> none  [the longest x4 10.9 us: rotate_pairs(): jnp.roll(values, 1, axis=-1)]
    convert_element_type x5 -> x0, other arithmetic: 12.1 us -> none  [the longest x1 8.46 us: prepare_rotated(): rotate_pairs(rms_scale(values, gain_vector), cosine_table, sine_table)]
    while x5 -> x0, local copies, waits for them, and re-layouts: 9.97 us -> none  [the longest x1 9.55 us: body(): attended = lax.map(attend_packed, (queries, key_rows, value_rows, masks))]
  transfers between devices with their start and end apart: 6 -> 0, of which waited for: 4 -> 0; matrix products, arithmetic and copies ran while one was open for 18% -> 0% of each run, Pallas kernels for 0% -> 0%
where the time goes in v1:
time: 121 us; the launch traced here: 119 us
  Pallas kernels  114 us (94%)
  local copies, waits for them, and re-layouts  4.01 us (3%)
    pallas_call x1, Pallas kernels, body(): pl.pallas_call(functools.partial(kernel, n, heads, chunk, group), out_sha...  114 us
    unnamed x7, local copies, waits for them, and re-layouts  4.01 us

profile of v1, /device:TPU:11, one launch (start us, length us, event | category | flops | bytes accessed | tf_op | source)
XLA Modules:
  0.0 118.9 jit_solution(17895841798975790476)
XLA Ops:
  0.6 114.2 %shard_map.157 = (bf16[128,3072]{1,0:T(8,128)(2,1)}, bf16[2,128,3072]{2,1,0:T(8,128)(2,1)}, bf16[2,16,3072]{2,1,0:T(8,128)(2,1)}) custom-call(bf16[32,128,128]{2,1,0:T(8,128)(2,1)} %bitcast.8, bf16[32,128,128]{2,1,0:T(8,128)(2,1)} %bitcast.9, bf16[32,128,128]{2,1,0:T(8,128)(2,1)} %bitcast.10, bf16[32,16,128]{2,1,0:T(8,128)(2,1)} %bitcast.11, ...), custom_call_target="tpu_custom_call" | custom-call | tf_op jit(solution)/shard_map/pallas_call | solution.py:332
  114.9 0.0 copy-start
  114.9 2.2 %copy.20 = bf16[128,3072]{1,0:T(8,128)(2,1)} copy(bf16[128,3072]{1,0:T(8,128)(2,1)} %get-tuple-element.6) | data formatting | bytes 1572864
  117.1 0.0 copy-done
  117.1 0.0 copy-start.1
  117.1 1.1 copy.21
  118.2 0.0 copy-done.1
  118.2 0.7 copy.22
Async XLA Ops:
  114.9 2.2 %copy-start = (bf16[2,128,3072]{2,1,0:T(8,128)(2,1)S(1)}, bf16[2,128,3072]{2,1,0:T(8,128)(2,1)}, u32[]{:S(2)}) copy-start(bf16[2,128,3072]{2,1,0:T(8,128)(2,1)} %get-tuple-element.7) | copy-start | bytes 4718596
  117.1 1.1 copy-start.1

commit v2 on v1

--- a/solution.py
+++ b/solution.py
@@ -47,23 +47,24 @@
     heads,
     chunk,
     group,
-    vq_ref,
-    vk_ref,
-    vv_ref,
-    tq_ref,
-    tk_ref,
-    tv_ref,
+    vv_hbm,
+    tv_hbm,
+    vk_hbm,
+    tk_hbm,
+    vq_hbm,
+    tq_hbm,
     pos_ref,
     len_ref,
     qg_ref,
     kg_ref,
     weight_hbm,
-    gate_ref,
-    vstream_hbm,
-    tstream_hbm,
-    guided_ref,
-    vnext_ref,
-    tnext_ref,
+    proj_hbm,
+    vv_ref,
+    tv_ref,
+    vk_ref,
+    tk_ref,
+    vq_ref,
+    tq_ref,
     comb,
     got,
     osend,
@@ -71,12 +72,11 @@
     vext,
     tables,
     weight,
-    vstream,
-    tstream,
     acc,
     send_sem,
     recv_sem,
     local_sem,
+    out_sem,
 ):
     me = lax.axis_index("sp")
     items, rows_v, head_dim = vq_ref.shape
@@ -93,13 +93,22 @@
             barrier, inc=1, device_id={"sp": lax.rem(me + i, n)}, device_id_type=MESH
         )
 
-    loads = (
-        pltpu.make_async_copy(weight_hbm, weight, local_sem.at[0]),
-        pltpu.make_async_copy(vstream_hbm, vstream, local_sem.at[1]),
-        pltpu.make_async_copy(tstream_hbm, tstream, local_sem.at[2]),
-    )
-    for load in loads:
+    sources = (vv_hbm, tv_hbm, vk_hbm, tk_hbm, vq_hbm, tq_hbm, weight_hbm)
+    places = (vv_ref, tv_ref, vk_ref, tk_ref, vq_ref, tq_ref, weight)
+    loads = [
+        pltpu.make_async_copy(there, here, local_sem.at[i])
+        for i, (there, here) in enumerate(zip(sources, places))
+    ]
+    for load in loads[:6]:
         load.start()
+
+    half = n // 2
+    side = me // half
+
+    def far_first(i, size):
+        blocks = half // size
+        other = lax.rem(side + 1 + i // blocks, 2)
+        return (other * blocks + lax.rem(me // size + i, blocks)) * size
 
     def copy_in(kind, wave, owner, target):
         return pltpu.make_async_remote_copy(
@@ -124,7 +133,7 @@
     def deal(kind, wave, make):
         @pl.loop(0, n)
         def _(i):
-            target = lax.rem(me + i, n)
+            target = far_first(i, 1)
             video, text = make(wave * n + target)
 
             def put(ref):
@@ -171,10 +180,12 @@
 
         return make
 
+    loads[0].wait()
+    loads[1].wait()
     pl.semaphore_wait(barrier, n - 1)
     deal(V, 0, make_value)
 
-    query_gain = qg_ref[...] * (head_dim ** (-0.5) * math.log2(math.e))
+    query_gain = qg_ref[...]
     key_gain = kg_ref[...]
     cosine, sine = rope_tables(pos_ref[...], head_dim)
     for slot, gain in ((0, key_gain), (1, query_gain)):
@@ -184,6 +195,9 @@
 
     make_key = make_normed(vk_ref, tk_ref, 0, key_gain)
     make_query = make_normed(vq_ref, tq_ref, 1, query_gain)
+    for load in loads[2:6]:
+        load.wait()
+    loads[6].start()
     for wave in range(waves):
         if wave > 0:
             deal(V, wave, make_value)
@@ -192,6 +206,7 @@
 
     acc[...] = jnp.zeros_like(acc)
 
+    score_scale = head_dim ** (-0.5) * math.log2(math.e)
     row = lax.broadcasted_iota(jnp.int32, (rows, 1), 0)
     for wave in range(waves):
         limit = len_ref[(wave * n + me) // heads]
@@ -211,7 +226,7 @@
 
         @pl.loop(0, n // chunk)
         def _(step):
-            first = lax.rem(me // chunk + step, n // chunk) * chunk
+            first = far_first(step, chunk)
             for j in range(chunk):
 
                 @pl.when(first + j != me)
@@ -223,7 +238,7 @@
             scores = lax.dot_general(
                 queries, keys, (((1,), (1,)), ((), ())), preferred_element_type=F32
             )
-            weights = jnp.exp2(scores).astype(BF16)
+            weights = jnp.exp2(scores * score_scale).astype(BF16)
             summed = jnp.dot(
                 weights, vext[...].reshape(n * rows, 2 * head_dim), preferred_element_type=F32
             )
@@ -240,13 +255,25 @@
                     osend[wave, first + j] = part
                     copy_back(wave, me, first + j).start()
 
-    loads[0].wait()
+    loads[6].wait()
     tile = math.gcd(width, 768)
-    for wave in range(waves):
-
-        @pl.loop(0, n // group)
+    count = heads // group
+
+    def write(branch, t):
+        columns = pl.ds(pl.multiple_of(t * tile, tile), tile)
+        return pltpu.make_async_copy(
+            acc.at[branch, :, columns], proj_hbm.at[branch, :, columns], out_sem.at[branch, t]
+        )
+
+    for branch in range(items // heads):
+        wave, start = divmod(branch * heads, n)
+
+        @pl.loop(0, count)
         def _(step):
-            first = lax.rem(me // group + n // group - step, n // group) * group
+            if count * group == n:
+                first = far_first(step, group)
+            else:
+                first = start + step * group
             for j in range(group):
 
                 @pl.when(first + j != me)
@@ -254,7 +281,7 @@
                     copy_back(wave, first + j, me).wait_recv()
 
             item = wave * n + first
-            branch, head = item // heads, lax.rem(item, heads)
+            head = item - branch * heads
             rows_in = jnp.concatenate([ohome[item + j] for j in range(group)], axis=1)
 
             @pl.loop(0, width // tile)
@@ -265,27 +292,9 @@
                     rows_in, weight[depth, columns], preferred_element_type=F32
                 )
 
-    loads[1].wait()
-    loads[2].wait()
-
-    @pl.loop(0, width // tile)
-    def _(t):
-        columns = pl.ds(pl.multiple_of(t * tile, tile), tile)
-        streams = []
-        for branch in range(2):
-            gate = gate_ref[pl.ds(branch, 1), columns]
-            stream = vstream[branch, :, columns].astype(F32) + gate * acc[
-                branch, pl.ds(0, rows_v), columns
-            ]
-            vnext_ref[branch, :, columns] = stream.astype(BF16)
-            streams.append(stream)
-            tnext_ref[branch, :, columns] = (
-                tstream[branch, :, columns].astype(F32)
-                + gate * acc[branch, pl.ds(rows_v, rows_t), columns]
-            ).astype(BF16)
-        guided_ref[:, columns] = (
-            streams[1] + guidance_scale * (streams[0] - streams[1])
-        ).astype(BF16)
+                @pl.when(step == count - 1)
+                def _():
+                    write(branch, t).start()
 
     for wave in range(waves):
 
@@ -295,6 +304,24 @@
             for kind in (V, K, Q):
                 copy_in(kind, wave, me, target).wait_send()
             copy_back(wave, me, target).wait_send()
+
+    for branch in range(items // heads):
+        for t in range(width // tile):
+            write(branch, t).wait()
+
+
+def finish(proj_ref, gate_ref, vstream_ref, tstream_ref, guided_ref, vnext_ref, tnext_ref):
+    rows_v, rows_t = vstream_ref.shape[1], tstream_ref.shape[1]
+    streams = []
+    for branch in range(2):
+        gate = gate_ref[branch : branch + 1, :]
+        stream = vstream_ref[branch].astype(F32) + gate * proj_ref[branch, :rows_v]
+        vnext_ref[branch] = stream.astype(BF16)
+        streams.append(stream)
+        tnext_ref[branch] = (
+            tstream_ref[branch].astype(F32) + gate * proj_ref[branch, rows_v : rows_v + rows_t]
+        ).astype(BF16)
+    guided_ref[...] = (streams[1] + guidance_scale * (streams[0] - streams[1])).astype(BF16)
 
 
 def body(
@@ -329,16 +356,18 @@
     vmem = pl.BlockSpec(memory_space=pltpu.VMEM)
     smem = pl.BlockSpec(memory_space=pltpu.SMEM)
     anywhere = pl.BlockSpec(memory_space=pl.ANY)
-    return pl.pallas_call(
+    tile = math.gcd(width, 768)
+    projected = pl.pallas_call(
         functools.partial(kernel, n, heads, chunk, group),
-        out_shape=(
-            jax.ShapeDtypeStruct((rows_v, width), BF16),
-            jax.ShapeDtypeStruct((branches, rows_v, width), BF16),
-            jax.ShapeDtypeStruct((branches, rows_t, width), BF16),
-        ),
-        in_specs=[vmem] * 7 + [smem, vmem, vmem, anywhere, vmem, anywhere, anywhere],
-        out_specs=(vmem, vmem, vmem),
+        out_shape=jax.ShapeDtypeStruct((branches, rows, width), F32),
+        in_specs=[anywhere] * 6 + [vmem, smem, vmem, vmem, anywhere],
+        out_specs=anywhere,
         scratch_shapes=[
+            pltpu.VMEM((items, rows_v, head_dim), BF16),
+            pltpu.VMEM((items, rows_t, head_dim), BF16),
+        ]
+        * 3
+        + [
             pltpu.VMEM((3, items, rows, head_dim), BF16),
             pltpu.VMEM((3, waves, n, rows, head_dim), BF16),
             pltpu.VMEM((waves, n, rows, head_dim), BF16),
@@ -346,32 +375,48 @@
             pltpu.VMEM((n, rows, 2 * head_dim), BF16),
             pltpu.VMEM((2, 2, rows_v, head_dim), F32),
             pltpu.VMEM(out_weight.shape, BF16),
-            pltpu.VMEM(video_stream.shape, BF16),
-            pltpu.VMEM(text_stream.shape, BF16),
             pltpu.VMEM((branches, rows, width), F32),
             pltpu.SemaphoreType.DMA((4, waves, n)),
             pltpu.SemaphoreType.DMA((4, waves, n)),
-            pltpu.SemaphoreType.DMA((3,)),
+            pltpu.SemaphoreType.DMA((7,)),
+            pltpu.SemaphoreType.DMA((branches, width // tile)),
         ],
         compiler_params=pltpu.CompilerParams(
             collective_id=0, has_side_effects=True, vmem_limit_bytes=63 * 1024 * 1024
         ),
     )(
+        flat(video_value),
+        flat(text_value),
+        flat(video_key),
+        flat(text_key),
         flat(video_query),
-        flat(video_key),
-        flat(video_value),
         flat(text_query),
-        flat(text_key),
-        flat(text_value),
         positions,
         text_lengths,
         query_gain.reshape(1, head_dim),
         key_gain.reshape(1, head_dim),
         out_weight,
-        branch_gates,
-        video_stream,
-        text_stream,
     )
+
+    def columns(*lead):
+        return pl.BlockSpec(lead + (tile,), lambda t: (0,) * len(lead) + (t,))
+
+    return pl.pallas_call(
+        finish,
+        grid=(width // tile,),
+        out_shape=(
+            jax.ShapeDtypeStruct((rows_v, width), BF16),
+            jax.ShapeDtypeStruct((branches, rows_v, width), BF16),
+            jax.ShapeDtypeStruct((branches, rows_t, width), BF16),
+        ),
+        in_specs=[
+            columns(branches, rows),
+            columns(branches),
+            columns(branches, rows_v),
+            columns(branches, rows_t),
+        ],
+        out_specs=(columns(rows_v), columns(branches, rows_v), columns(branches, rows_t)),
+    )(projected, branch_gates, video_stream, text_stream)
 
 
 def solution(mesh):

time: 121 us -> 123 us (1.017)
  the two profiles are of different devices: /device:TPU:11 before, /device:TPU:0 now
where the time goes in v2:
time: 123 us
  Pallas kernels  122 us (99%)
    pallas_call x1, Pallas kernels, body(): pl.pallas_call(functools.partial(kernel, n, heads, chunk, group), out_sha...  117 us
    pallas_call x1, Pallas kernels, body(): pl.pallas_call(finish, grid=(width // tile,), out_shape=(jax.ShapeDtypeSt...  4.57 us

profile of v2, /device:TPU:0, one launch (start us, length us, event | category | flops | bytes accessed | tf_op | source)
XLA Modules:
  0.0 122.6 jit_solution(3545662848577738104)
XLA Ops:
  0.6 117.4 %shard_map.157.proj_ref = f32[2,144,3072]{2,1,0:T(8,128)} custom-call(bf16[32,128,128]{2,1,0:T(8,128)(2,1)} %bitcast.8, bf16[32,16,128]{2,1,0:T(8,128)(2,1)} %bitcast.11, bf16[32,128,128]{2,1,0:T(8,128)(2,1)} %bitcast.9, bf16[32,16,128]{2,1,0:T(8,128)(2,1)} %bitcast.12, bf16[32,128,128]{2,1,0:T(8,128)(2,1)} %bitcast.10, bf16[32,16,128]{2,1,0:T(8,128)(2,1)} %bitcast.13, ...), custom_call_target="tpu_custom_call" | custom-call | tf_op jit(solution)/shard_map/pallas_call | solution.py:360
  118.0 4.6 %shard_map.158 = (bf16[128,3072]{1,0:T(8,128)(2,1)}, bf16[2,128,3072]{2,1,0:T(8,128)(2,1)}, bf16[2,16,3072]{2,1,0:T(8,128)(2,1)}) custom-call(f32[2,144,3072]{2,1,0:T(8,128)} %shard_map.157.proj_ref, f32[2,3072]{1,0:T(2,128)} %gate_ref.1, bf16[2,128,3072]{2,1,0:T(8,128)(2,1)} %vstream_ref.1, bf16[2,16,3072]{2,1,0:T(8,128)(2,1)} %tstream_ref.1), custom_call_target="tpu_custom_call" | custom-call | tf_op jit(solution)/shard_map/pallas_call | solution.py:404

commit v3 on v2

--- a/solution.py
+++ b/solution.py
@@ -102,14 +102,6 @@
     for load in loads[:6]:
         load.start()
 
-    half = n // 2
-    side = me // half
-
-    def far_first(i, size):
-        blocks = half // size
-        other = lax.rem(side + 1 + i // blocks, 2)
-        return (other * blocks + lax.rem(me // size + i, blocks)) * size
-
     def copy_in(kind, wave, owner, target):
         return pltpu.make_async_remote_copy(
             src_ref=comb.at[kind, wave * n + target],
@@ -133,7 +125,7 @@
     def deal(kind, wave, make):
         @pl.loop(0, n)
         def _(i):
-            target = far_first(i, 1)
+            target = lax.rem(me + i, n)
             video, text = make(wave * n + target)
 
             def put(ref):
@@ -226,7 +218,7 @@
 
         @pl.loop(0, n // chunk)
         def _(step):
-            first = far_first(step, chunk)
+            first = lax.rem(me // chunk + step, n // chunk) * chunk
             for j in range(chunk):
 
                 @pl.when(first + j != me)
@@ -271,7 +263,7 @@
         @pl.loop(0, count)
         def _(step):
             if count * group == n:
-                first = far_first(step, group)
+                first = lax.rem(me // group + n // group - 1 - step + count, count) * group
             else:
                 first = start + step * group
             for j in range(group):
@@ -398,12 +390,14 @@
         out_weight,
     )
 
+    step = math.gcd(width, 512)
+
     def columns(*lead):
-        return pl.BlockSpec(lead + (tile,), lambda t: (0,) * len(lead) + (t,))
+        return pl.BlockSpec(lead + (step,), lambda t: (0,) * len(lead) + (t,))
 
     return pl.pallas_call(
         finish,
-        grid=(width // tile,),
+        grid=(width // step,),
         out_shape=(
             jax.ShapeDtypeStruct((rows_v, width), BF16),
             jax.ShapeDtypeStruct((branches, rows_v, width), BF16),

time: 123 us -> 120 us (0.976)
  the two profiles are of different devices: /device:TPU:0 before, /device:TPU:11 now
where the time goes in v3:
time: 120 us; the launch traced here: 118 us
  Pallas kernels  118 us (98%)
    pallas_call x1, Pallas kernels, body(): pl.pallas_call(functools.partial(kernel, n, heads, chunk, group), out_sha...  112 us
    pallas_call x1, Pallas kernels, body(): pl.pallas_call(finish, grid=(width // step,), out_shape=(jax.ShapeDtypeSt...  5.62 us

profile of v3, /device:TPU:11, one launch (start us, length us, event | category | flops | bytes accessed | tf_op | source)
XLA Modules:
  0.0 118.3 jit_solution(12532999189192612823)
XLA Ops:
  0.6 112.0 %shard_map.157.proj_ref = f32[2,144,3072]{2,1,0:T(8,128)} custom-call(bf16[32,128,128]{2,1,0:T(8,128)(2,1)} %bitcast.8, bf16[32,16,128]{2,1,0:T(8,128)(2,1)} %bitcast.11, bf16[32,128,128]{2,1,0:T(8,128)(2,1)} %bitcast.9, bf16[32,16,128]{2,1,0:T(8,128)(2,1)} %bitcast.12, bf16[32,128,128]{2,1,0:T(8,128)(2,1)} %bitcast.10, bf16[32,16,128]{2,1,0:T(8,128)(2,1)} %bitcast.13, ...), custom_call_target="tpu_custom_call" | custom-call | tf_op jit(solution)/shard_map/pallas_call | solution.py:352
  112.6 5.6 %shard_map.158 = (bf16[128,3072]{1,0:T(8,128)(2,1)}, bf16[2,128,3072]{2,1,0:T(8,128)(2,1)}, bf16[2,16,3072]{2,1,0:T(8,128)(2,1)}) custom-call(f32[2,144,3072]{2,1,0:T(8,128)} %shard_map.157.proj_ref, f32[2,3072]{1,0:T(2,128)} %gate_ref.1, bf16[2,128,3072]{2,1,0:T(8,128)(2,1)} %vstream_ref.1, bf16[2,16,3072]{2,1,0:T(8,128)(2,1)} %tstream_ref.1), custom_call_target="tpu_custom_call" | custom-call | tf_op jit(solution)/shard_map/pallas_call | solution.py:398
